TPU v7x, 32 devices: a whole 2x2x4 slice. The times are simulated.
32 devices in a mesh: samp: 4 (over z), seq: 8 (over y, x, core).
Axes of the slice: x: 2, y: 2, z: 4, core: 2. Of those that a mesh axis runs over, the one named last changes fastest.
Arguments:
- queries: bfloat16 [4, 4096, 3584], P('samp', 'seq'), may hold values from -200 to 200
- keys: bfloat16 [4, 4096, 512], P('samp', 'seq'), may hold values from -6 to 6
- values: bfloat16 [4, 4096, 512], P('samp', 'seq'), may hold values from -6 to 6
- reg_owner: int32 [4], P('samp'), may hold values from 0 to 7
- block_lists: int32 [4, 32, 8], P('samp', 'seq'), may hold values from 0 to 31, as said below
- list_counts: int32 [4, 32], P('samp', 'seq'), may hold values from 0 to 8, as said below
- image_blocks: int32 [4, 32], P('samp', 'seq'), may hold values from 0 to 1, as said below
Outputs:
- attended: bfloat16 [4, 4096, 3584], P('samp', 'seq')
Inputs may be any that keep to these rules, and one draw needn't show every extreme that they name: `block_lists`: block b lies on sequence index b // 4. Entry t of a list is used only where t < the block's count, unused entries are 0. The used entries of one block name blocks of distinct sequence indices other than its own. Over all blocks of one sequence index, at most one distinct block of each other sequence index is named. On the last sequence index of each sample, the lists together name a block of every other index. `list_counts`: 0 for image blocks; at most 8. `image_blocks`: the blocks of the last sequence index of each sample are text blocks.
All inputs are finite; a program needn't handle non-finite values.
Results may differ from a plain program's by a relative error of at most 0.0043.
Values may be sent and summed in bfloat16 or wider, within the bound.
No kernel may reach another device: no remote copies, remote signals or barrier semaphores. Data moves between devices by JAX's collectives and lax.ppermute only.
A program may use at most 128 MiB of HBM per device.

v0:
```python
import math
import jax
import jax.numpy as jnp
from jax import lax
from jax.sharding import PartitionSpec as P

QUERY_HEADS = 28
KEY_VALUE_HEADS = 4
HEAD_SIZE = 128
REG = 64
very_low = -1e30


def broadcast(value, axis, source):
    kept = jnp.where(lax.axis_index(axis) == source, value, 0).astype(value.dtype)
    return lax.psum(kept, axis)


def group_part(query_row_list, key_row_list, value_row_list, visible):
    head_grouped = query_row_list.reshape(
        query_row_list.shape[0], KEY_VALUE_HEADS, QUERY_HEADS // KEY_VALUE_HEADS, HEAD_SIZE
    )
    per_head_keys = key_row_list.reshape(-1, KEY_VALUE_HEADS, HEAD_SIZE)
    per_head_values = value_row_list.reshape(-1, KEY_VALUE_HEADS, HEAD_SIZE)
    scores = jnp.einsum(
        "qhgd,khd->hgqk", head_grouped, per_head_keys, preferred_element_type=jnp.float32
    ) / math.sqrt(HEAD_SIZE)
    scores = jnp.where(visible, scores, very_low)
    maxima = jnp.max(scores, axis=-1)
    weights = jnp.where(visible, jnp.exp(scores - maxima[..., None]), 0.0)
    totals = jnp.sum(weights, axis=-1)
    partial_value = jnp.einsum(
        "hgqk,khd->hgqd",
        weights.astype(jnp.bfloat16),
        per_head_values,
        preferred_element_type=jnp.float32,
    )
    return (maxima, totals, partial_value)


def combine(parts):
    top_score = jnp.maximum(jnp.maximum(parts[0][0], parts[1][0]), parts[2][0])
    numerator = jnp.zeros(parts[0][2].shape, jnp.float32)
    denominator = jnp.zeros(parts[0][1].shape, jnp.float32)
    for maxima, totals, partial_value in parts:
        rescale = jnp.exp(maxima - top_score)
        numerator = numerator + rescale[..., None] * partial_value
        denominator = denominator + rescale * totals
    merged = numerator / denominator[..., None]
    return merged.transpose(2, 0, 1, 3).reshape(merged.shape[2], -1)


def per_device(queries, keys, values, reg_owner, block_lists, list_counts, image_blocks):
    query_all = queries[0]
    every_key = keys[0]
    every_value = values[0]
    local_lists = block_lists[0]
    local_counts = list_counts[0]
    local_image = image_blocks[0]
    devices = lax.axis_size("seq")
    position = lax.axis_index("seq")
    blocks_here = local_lists.shape[0]
    slot_count = local_lists.shape[1]
    rows_block = every_key.shape[0] // blocks_here
    kv_width = every_key.shape[1]
    stacked = jnp.stack([every_key[:REG], every_value[:REG]])
    registers = broadcast(stacked, "seq", reg_owner[0])
    reg_keys = registers[0]
    reg_values = registers[1]
    all_lists, all_counts = (
        lax.all_gather(local_lists, "seq", axis=0, tiled=True),
        lax.all_gather(local_counts, "seq", axis=0, tiled=True),
    )
    own_ids = position * blocks_here + jnp.arange(blocks_here, dtype=jnp.int32)
    live_slots = jnp.arange(slot_count, dtype=jnp.int32)[None, :] < all_counts[:, None]
    named_here = (all_lists[:, :, None] == own_ids[None, None, :]) & live_slots[:, :, None]
    wanted = jnp.any(named_here, axis=1).reshape(devices, blocks_here, blocks_here)
    selector = jnp.any(wanted, axis=1).astype(jnp.bfloat16)
    send_keys = jnp.dot(
        selector,
        every_key.reshape(blocks_here, rows_block * kv_width),
        preferred_element_type=jnp.float32,
    ).astype(jnp.bfloat16)
    send_values = jnp.dot(
        selector,
        every_value.reshape(blocks_here, rows_block * kv_width),
        preferred_element_type=jnp.float32,
    ).astype(jnp.bfloat16)
    owners = (local_lists // blocks_here).reshape(-1)
    got_keys, got_values = (
        lax.all_to_all(
            send_keys.reshape(devices, rows_block, kv_width),
            "seq",
            split_axis=0,
            concat_axis=0,
            tiled=True,
        ),
        lax.all_to_all(
            send_values.reshape(devices, rows_block, kv_width),
            "seq",
            split_axis=0,
            concat_axis=0,
            tiled=True,
        ),
    )
    remote_keys = got_keys[owners]
    remote_values = got_values[owners]
    remote_keys = remote_keys.reshape(blocks_here, slot_count * rows_block, kv_width)
    remote_values = remote_values.reshape(blocks_here, slot_count * rows_block, kv_width)
    row_ids = jnp.arange(rows_block)
    slot_rows = jnp.arange(slot_count * rows_block) // rows_block

    def attend(pieces):
        query_row_list, own_keys, own_values, named_keys, named_values, list_count, is_image = (
            pieces
        )
        reg_visible = jnp.ones((rows_block, reg_keys.shape[0]), bool)
        own_visible = (row_ids[None, :] <= row_ids[:, None]) | (is_image == 1)
        far_visible = jnp.broadcast_to(
            slot_rows[None, :] < list_count, (rows_block, slot_count * rows_block)
        )
        parts = [
            group_part(query_row_list, reg_keys, reg_values, reg_visible),
            group_part(query_row_list, own_keys, own_values, own_visible),
            group_part(query_row_list, named_keys, named_values, far_visible),
        ]
        return combine(parts).astype(jnp.bfloat16)

    blocks_out = lax.map(
        attend,
        (
            query_all.reshape(blocks_here, rows_block, -1),
            every_key.reshape(blocks_here, rows_block, kv_width),
            every_value.reshape(blocks_here, rows_block, kv_width),
            remote_keys,
            remote_values,
            local_counts,
            local_image,
        ),
    )
    return blocks_out.reshape(1, blocks_here * rows_block, -1)


def solution(mesh):
    placed = (
        P("samp", "seq", None),
        P("samp", "seq", None),
        P("samp", "seq", None),
        P("samp"),
        P("samp", "seq", None),
        P("samp", "seq"),
        P("samp", "seq"),
    )
    return jax.shard_map(
        per_device, mesh=mesh, in_specs=placed, out_specs=P("samp", "seq", None), check_vma=False
    )
```

profile of v0, /device:TPU:0, one launch (start us, length us, event | category | flops | bytes accessed | tf_op | source)
XLA Modules:
  0.0 281.8 jit_solution(2486919620880724648)
XLA Ops:
  9.2 9.5 %all-reduce = s32[32]{0:T(128)S(1)} all-reduce(s32[32]{0:T(128)S(1)} %bitcast_dynamic-update-slice_fusion), channel_id=3, replica_groups=mesh['samp'=4,'seq'=8] {'seq'}, use_global_device_ids=true, to_apply=%add | all-reduce | flops 32 | bytes 256
  18.8 8.3 %all-gather = s32[1,32,8]{2,0,1:T(1,128)S(1)} all-gather(s32[1,4,8]{2,0,1:T(1,128)} %bitcast.266), channel_id=2, replica_groups=mesh['samp'=4,'seq'=8] {'seq'}, dimensions={1}, use_global_device_ids=true | all-gather | bytes 1152 | tf_op jit(solution)/shard_map/all_gather | solution.py:71
  30.7 3.6 %all-to-all-start = ((bf16[8,128,512]{2,1,0:T(8,128)(2,1)}), bf16[8,128,512]{2,1,0:T(8,128)(2,1)S(1)}, u32[]{:S(2)}, u32[]{:S(2)}) async-start(bf16[8,128,512]{2,1,0:T(8,128)(2,1)} %copy.75), calls=%async_computation | async-start | bytes 2097152 | tf_op jit(solution)/shard_map/all_to_all | solution.py:91
  36.5 13.1 %all-to-all-done = bf16[8,128,512]{2,1,0:T(8,128)(2,1)S(1)} async-done(((bf16[8,128,512]{2,1,0:T(8,128)(2,1)}), bf16[8,128,512]{2,1,0:T(8,128)(2,1)S(1)}, u32[]{:S(2)}, u32[]{:S(2)}) %all-to-all-start) | async-done | bytes 1048608 | tf_op jit(solution)/shard_map/all_to_all | solution.py:91
  49.6 3.6 %all-to-all-start.1 = ((bf16[8,128,512]{2,1,0:T(8,128)(2,1)}), bf16[8,128,512]{2,1,0:T(8,128)(2,1)S(1)}, u32[]{:S(2)}, u32[]{:S(2)}) async-start(bf16[8,128,512]{2,1,0:T(8,128)(2,1)} %copy.76), calls=%async_computation.1 | async-start | bytes 2097152 | tf_op jit(solution)/shard_map/all_to_all | solution.py:98
  54.8 57.3 %all-reduce.3.cloned.1.call-done = bf16[2,64,512]{2,1,0:T(8,128)(2,1)} async-done(((bf16[2,64,512]{2,1,0:T(8,128)(2,1)}), bf16[2,64,512]{2,1,0:T(8,128)(2,1)}) %all-reduce.3.cloned.1.call-update) | async-done | bytes 131088 | tf_op jit(solution)/shard_map/psum | solution.py:16
  117.1 2.8 %gather_fusion.1 = bf16[32,128,512]{2,1,0:T(8,128)(2,1)} fusion(bf16[8,128,512]{2,1,0:T(8,128)(2,1)S(1)} %all-to-all-done.1, s32[1024]{0:T(1024)S(1)} %pad_clamp_fusion), kind=kCustom, calls=%fused_computation.1 | custom fusion | bytes 8388736 | tf_op jit(solution)/shard_map/gather | solution.py:107
  120.0 155.0 %while.12 = (s32[]{:T(128)}, bf16[4,128,3584]{2,1,0:T(8,128)(2,1)}, bf16[4,128,3584]{2,1,0:T(8,128)(2,1)}, bf16[1,64,512]{2,1,0:T(8,128)(2,1)}, s32[4]{0:T(128)S...) while((s32[]{:T(128)}, bf16[4,128,3584]{2,1,0:T(8,128)(2,1)}, ...), condition=%wide.wide.region_10.11_spmd.clone, body=%wide.wide.region_3.10_spmd.clone.sunk | while | flops 2289687552 | bytes 161137776 | solution.py:129
  124.2 3.0 %constant_dynamic-slice_fusion.13 = (bf16[1,1024,512]{2,1,0:T(8,128)(2,1)}, bf16[1,1024,512]{2,1,0:T(8,128)(2,1)}) fusion(bf16[4,1024,512]{2,1,0:T(8,128)(2,1)} %get-tuple-element.384, s32[]{:T(128)} %get-tuple-element.359, bf16[4,1024,512]{2,1,0:T(8,128)(2,1)} %get-tuple-element.381), kind=kLoop, calls=%fused_computation.65.clone.clone.1 | loop fusion | bytes 4194308 | tf_op jit(solution)/shard_map/while/body/jit(dynamic_index_in_dim)/dynamic_slice | solution.py:129
  130.8 4.4 %bitcast_reduce_fusion.3 = (f32[4,7,128]{2,1,0:T(8,128)S(1)}, f32[4,1024,128,7]{2,1,3,0:T(8,128)S(1)}) fusion(pred[1024]{0:T(1024)(128)(4,1)S(1)} %fusion.129, bf16[1024,4,128,1]{0,2,3,1:T(8,128)(2,1)} %bitcast.250, bf16[128,4,7,128]{0,3,2,1:T(8,128)(2,1)S(1)} %bitcast.248), kind=kOutput, calls=%fused_computation.5.clone.clone.1 | convolution fusion | flops 950530560 | bytes 16661504 | tf_op jit(solution)/shard_map/while/body/eval_jaxpr/qhgd,khd->hgqk/dot_general | solution.py:25
  135.2 4.2 %fusion.130 = f32[4,7,128]{2,1,0:T(8,128)S(1)} fusion(f32[4,1024,128,7]{2,1,3,0:T(8,128)S(1)} %get-tuple-element.338, f32[4,7,128]{2,1,0:T(8,128)S(1)} %get-tuple-element.339, pred[1024]{0:T(1024)(128)(4,1)S(1)} %fusion.129), kind=kLoop, calls=%fused_computation.9.clone.clone.1 | loop fusion | flops 18346496 | bytes 14709760 | tf_op jit(solution)/shard_map/while/body/eval_jaxpr/reduce_sum | solution.py:31
  147.1 9.1 %fusion.134 = bf16[128,4,7,128]{0,3,2,1:T(8,128)(2,1)} fusion(f32[4,7,128,128]{2,3,1,0:T(8,128)S(1)} %copy-done.3, f32[4,7,128,128]{2,3,1,0:T(8,128)} %fusion.128, bf16[1024,4,128,1]{0,2,3,1:T(8,128)(2,1)S(1)} %bitcast.251, f32[4,1024,128,7]{2,1,3,0:T(8,128)} %copy-done, f32[4,7,128]{2,1,0:T(8,128)S(1)} %get-tuple-element.339, ...), kind=kOutput, calls=%fused_computation.17.clone.clone.1 | convolution fusion | flops 961085440 | bytes 20388864 | tf_op jit(solution)/shard_map/while/body/eval_jaxpr/hgqk,khd->hgqd/dot_general | solution.py:32
  162.9 3.0 %constant_dynamic-slice_fusion.13 = (bf16[1,1024,512]{2,1,0:T(8,128)(2,1)}, bf16[1,1024,512]{2,1,0:T(8,128)(2,1)}) fusion(bf16[4,1024,512]{2,1,0:T(8,128)(2,1)} %get-tuple-element.384, s32[]{:T(128)} %get-tuple-element.359, bf16[4,1024,512]{2,1,0:T(8,128)(2,1)} %get-tuple-element.381), kind=kLoop, calls=%fused_computation.65.clone.clone.1 | loop fusion | bytes 4194308 | tf_op jit(solution)/shard_map/while/body/jit(dynamic_index_in_dim)/dynamic_slice | solution.py:129
  169.5 4.4 %bitcast_reduce_fusion.3 = (f32[4,7,128]{2,1,0:T(8,128)S(1)}, f32[4,1024,128,7]{2,1,3,0:T(8,128)S(1)}) fusion(pred[1024]{0:T(1024)(128)(4,1)S(1)} %fusion.129, bf16[1024,4,128,1]{0,2,3,1:T(8,128)(2,1)} %bitcast.250, bf16[128,4,7,128]{0,3,2,1:T(8,128)(2,1)S(1)} %bitcast.248), kind=kOutput, calls=%fused_computation.5.clone.clone.1 | convolution fusion | flops 950530560 | bytes 16661504 | tf_op jit(solution)/shard_map/while/body/eval_jaxpr/qhgd,khd->hgqk/dot_general | solution.py:25
  174.0 4.2 %fusion.130 = f32[4,7,128]{2,1,0:T(8,128)S(1)} fusion(f32[4,1024,128,7]{2,1,3,0:T(8,128)S(1)} %get-tuple-element.338, f32[4,7,128]{2,1,0:T(8,128)S(1)} %get-tuple-element.339, pred[1024]{0:T(1024)(128)(4,1)S(1)} %fusion.129), kind=kLoop, calls=%fused_computation.9.clone.clone.1 | loop fusion | flops 18346496 | bytes 14709760 | tf_op jit(solution)/shard_map/while/body/eval_jaxpr/reduce_sum | solution.py:31
  185.8 9.1 %fusion.134 = bf16[128,4,7,128]{0,3,2,1:T(8,128)(2,1)} fusion(f32[4,7,128,128]{2,3,1,0:T(8,128)S(1)} %copy-done.3, f32[4,7,128,128]{2,3,1,0:T(8,128)} %fusion.128, bf16[1024,4,128,1]{0,2,3,1:T(8,128)(2,1)S(1)} %bitcast.251, f32[4,1024,128,7]{2,1,3,0:T(8,128)} %copy-done, f32[4,7,128]{2,1,0:T(8,128)S(1)} %get-tuple-element.339, ...), kind=kOutput, calls=%fused_computation.17.clone.clone.1 | convolution fusion | flops 961085440 | bytes 20388864 | tf_op jit(solution)/shard_map/while/body/eval_jaxpr/hgqk,khd->hgqd/dot_general | solution.py:32
  201.7 3.0 %constant_dynamic-slice_fusion.13 = (bf16[1,1024,512]{2,1,0:T(8,128)(2,1)}, bf16[1,1024,512]{2,1,0:T(8,128)(2,1)}) fusion(bf16[4,1024,512]{2,1,0:T(8,128)(2,1)} %get-tuple-element.384, s32[]{:T(128)} %get-tuple-element.359, bf16[4,1024,512]{2,1,0:T(8,128)(2,1)} %get-tuple-element.381), kind=kLoop, calls=%fused_computation.65.clone.clone.1 | loop fusion | bytes 4194308 | tf_op jit(solution)/shard_map/while/body/jit(dynamic_index_in_dim)/dynamic_slice | solution.py:129
  208.3 4.4 %bitcast_reduce_fusion.3 = (f32[4,7,128]{2,1,0:T(8,128)S(1)}, f32[4,1024,128,7]{2,1,3,0:T(8,128)S(1)}) fusion(pred[1024]{0:T(1024)(128)(4,1)S(1)} %fusion.129, bf16[1024,4,128,1]{0,2,3,1:T(8,128)(2,1)} %bitcast.250, bf16[128,4,7,128]{0,3,2,1:T(8,128)(2,1)S(1)} %bitcast.248), kind=kOutput, calls=%fused_computation.5.clone.clone.1 | convolution fusion | flops 950530560 | bytes 16661504 | tf_op jit(solution)/shard_map/while/body/eval_jaxpr/qhgd,khd->hgqk/dot_general | solution.py:25
  212.7 4.2 %fusion.130 = f32[4,7,128]{2,1,0:T(8,128)S(1)} fusion(f32[4,1024,128,7]{2,1,3,0:T(8,128)S(1)} %get-tuple-element.338, f32[4,7,128]{2,1,0:T(8,128)S(1)} %get-tuple-element.339, pred[1024]{0:T(1024)(128)(4,1)S(1)} %fusion.129), kind=kLoop, calls=%fused_computation.9.clone.clone.1 | loop fusion | flops 18346496 | bytes 14709760 | tf_op jit(solution)/shard_map/while/body/eval_jaxpr/reduce_sum | solution.py:31
  224.6 9.1 %fusion.134 = bf16[128,4,7,128]{0,3,2,1:T(8,128)(2,1)} fusion(f32[4,7,128,128]{2,3,1,0:T(8,128)S(1)} %copy-done.3, f32[4,7,128,128]{2,3,1,0:T(8,128)} %fusion.128, bf16[1024,4,128,1]{0,2,3,1:T(8,128)(2,1)S(1)} %bitcast.251, f32[4,1024,128,7]{2,1,3,0:T(8,128)} %copy-done, f32[4,7,128]{2,1,0:T(8,128)S(1)} %get-tuple-element.339, ...), kind=kOutput, calls=%fused_computation.17.clone.clone.1 | convolution fusion | flops 961085440 | bytes 20388864 | tf_op jit(solution)/shard_map/while/body/eval_jaxpr/hgqk,khd->hgqd/dot_general | solution.py:32
  240.4 3.0 %constant_dynamic-slice_fusion.13 = (bf16[1,1024,512]{2,1,0:T(8,128)(2,1)}, bf16[1,1024,512]{2,1,0:T(8,128)(2,1)}) fusion(bf16[4,1024,512]{2,1,0:T(8,128)(2,1)} %get-tuple-element.384, s32[]{:T(128)} %get-tuple-element.359, bf16[4,1024,512]{2,1,0:T(8,128)(2,1)} %get-tuple-element.381), kind=kLoop, calls=%fused_computation.65.clone.clone.1 | loop fusion | bytes 4194308 | tf_op jit(solution)/shard_map/while/body/jit(dynamic_index_in_dim)/dynamic_slice | solution.py:129
  247.0 4.4 %bitcast_reduce_fusion.3 = (f32[4,7,128]{2,1,0:T(8,128)S(1)}, f32[4,1024,128,7]{2,1,3,0:T(8,128)S(1)}) fusion(pred[1024]{0:T(1024)(128)(4,1)S(1)} %fusion.129, bf16[1024,4,128,1]{0,2,3,1:T(8,128)(2,1)} %bitcast.250, bf16[128,4,7,128]{0,3,2,1:T(8,128)(2,1)S(1)} %bitcast.248), kind=kOutput, calls=%fused_computation.5.clone.clone.1 | convolution fusion | flops 950530560 | bytes 16661504 | tf_op jit(solution)/shard_map/while/body/eval_jaxpr/qhgd,khd->hgqk/dot_general | solution.py:25
  251.4 4.2 %fusion.130 = f32[4,7,128]{2,1,0:T(8,128)S(1)} fusion(f32[4,1024,128,7]{2,1,3,0:T(8,128)S(1)} %get-tuple-element.338, f32[4,7,128]{2,1,0:T(8,128)S(1)} %get-tuple-element.339, pred[1024]{0:T(1024)(128)(4,1)S(1)} %fusion.129), kind=kLoop, calls=%fused_computation.9.clone.clone.1 | loop fusion | flops 18346496 | bytes 14709760 | tf_op jit(solution)/shard_map/while/body/eval_jaxpr/reduce_sum | solution.py:31
  263.3 9.1 %fusion.134 = bf16[128,4,7,128]{0,3,2,1:T(8,128)(2,1)} fusion(f32[4,7,128,128]{2,3,1,0:T(8,128)S(1)} %copy-done.3, f32[4,7,128,128]{2,3,1,0:T(8,128)} %fusion.128, bf16[1024,4,128,1]{0,2,3,1:T(8,128)(2,1)S(1)} %bitcast.251, f32[4,1024,128,7]{2,1,3,0:T(8,128)} %copy-done, f32[4,7,128]{2,1,0:T(8,128)S(1)} %get-tuple-element.339, ...), kind=kOutput, calls=%fused_computation.17.clone.clone.1 | convolution fusion | flops 961085440 | bytes 20388864 | tf_op jit(solution)/shard_map/while/body/eval_jaxpr/hgqk,khd->hgqd/dot_general | solution.py:32
  (201 shorter events, 82.7 us)
Async XLA Ops:
  6.5 27.7 %copy-start.4 = (bf16[1,512,512]{2,1,0:T(8,128)(2,1)S(1)}, bf16[1,512,512]{2,1,0:T(8,128)(2,1)}, u32[]{:S(2)}) copy-start(bf16[1,512,512]{2,1,0:T(8,128)(2,1)} %param.11) | copy-start | bytes 1572868
  30.7 18.9 %all-to-all-start = ((bf16[8,128,512]{2,1,0:T(8,128)(2,1)}), bf16[8,128,512]{2,1,0:T(8,128)(2,1)S(1)}, u32[]{:S(2)}, u32[]{:S(2)}) async-start(bf16[8,128,512]{2,1,0:T(8,128)(2,1)} %copy.75), calls=%async_computation | async-start | bytes 2097152 | tf_op jit(solution)/shard_map/all_to_all | solution.py:91
  34.2 19.8 %slice-start = ((bf16[1,512,512]{2,1,0:T(8,128)(2,1)}), bf16[1,64,512]{2,1,0:T(8,128)(2,1)S(1)}, s32[]{:S(2)}) async-start(bf16[1,512,512]{2,1,0:T(8,128)(2,1)} %param.11), calls=%async_computation.3 | async-start | bytes 131072 | tf_op jit(solution)/shard_map/slice | solution.py:66
  34.3 19.7 %slice-start.1 = ((bf16[1,512,512]{2,1,0:T(8,128)(2,1)}), bf16[1,64,512]{2,1,0:T(8,128)(2,1)S(1)}, s32[]{:S(2)}) async-start(bf16[1,512,512]{2,1,0:T(8,128)(2,1)} %param.10), calls=%async_computation.4 | async-start | bytes 131072 | tf_op jit(solution)/shard_map/slice | solution.py:66
  34.3 20.4 %copy-start.11 = (s32[1,4,8]{2,1,0:T(4,128)S(1)}, s32[1,4,8]{2,1,0:T(4,128)}, u32[]{:S(2)}) copy-start(s32[1,4,8]{2,1,0:T(4,128)} %param.13) | copy-start | bytes 388
  49.6 67.6 %all-to-all-start.1 = ((bf16[8,128,512]{2,1,0:T(8,128)(2,1)}), bf16[8,128,512]{2,1,0:T(8,128)(2,1)S(1)}, u32[]{:S(2)}, u32[]{:S(2)}) async-start(bf16[8,128,512]{2,1,0:T(8,128)(2,1)} %copy.76), calls=%async_computation.1 | async-start | bytes 2097152 | tf_op jit(solution)/shard_map/all_to_all | solution.py:98
  53.1 59.0 %all-reduce.3.cloned.1.call-start = ((), (), s32[]{:S(2)}) async-start(), calls=%async_computation.2 | async-start | bytes 262144 | tf_op jit(solution)/shard_map/psum | solution.py:16
  113.0 4.1 %copy-start.9 = (bf16[1,64,512]{2,1,0:T(8,128)(2,1)}, bf16[1,64,512]{2,1,0:T(8,128)(2,1)S(1)}, u32[]{:S(2)}) copy-start(bf16[1,64,512]{2,1,0:T(8,128)(2,1)S(1)} %get-tuple-element.352) | copy-start | bytes 196612
  113.0 4.1 %copy-start.10 = (bf16[1,64,512]{2,1,0:T(8,128)(2,1)}, bf16[1,64,512]{2,1,0:T(8,128)(2,1)S(1)}, u32[]{:S(2)}) copy-start(bf16[1,64,512]{2,1,0:T(8,128)(2,1)S(1)} %get-tuple-element.347) | copy-start | bytes 196612
  123.7 5.8 %copy-start.14 = (s32[4]{0:T(128)S(1)}, s32[4]{0:T(128)}, u32[]{:S(2)}) copy-start(s32[4]{0:T(128)} %get-tuple-element.380) | copy-start | bytes 52 | tf_op jit(solution)/shard_map/while
  135.2 5.2 %copy-start = (f32[4,1024,128,7]{2,1,3,0:T(8,128)}, f32[4,1024,128,7]{2,1,3,0:T(8,128)S(1)}, u32[]{:S(2)}) copy-start(f32[4,1024,128,7]{2,1,3,0:T(8,128)S(1)} %get-tuple-element.338) | copy-start | bytes 44040196 | tf_op jit(solution)/shard_map/while
  135.2 5.2 %copy-start.8 = (bf16[64,4,128]{2,1,0:T(4,128)(2,1)S(1)}, bf16[64,4,128]{2,1,0:T(4,128)(2,1)}, u32[]{:S(2)}) copy-start(bf16[64,4,128]{2,1,0:T(4,128)(2,1)} %get-tuple-element.385) | copy-start | bytes 196612 | tf_op jit(solution)/shard_map/while
  140.4 3.5 %copy-start.7 = (bf16[64,4,128]{2,1,0:T(4,128)(2,1)S(1)}, bf16[64,4,128]{2,1,0:T(4,128)(2,1)}, u32[]{:S(2)}) copy-start(bf16[64,4,128]{2,1,0:T(4,128)(2,1)} %get-tuple-element.386) | copy-start | bytes 196612 | tf_op jit(solution)/shard_map/while
  162.4 5.8 %copy-start.14 = (s32[4]{0:T(128)S(1)}, s32[4]{0:T(128)}, u32[]{:S(2)}) copy-start(s32[4]{0:T(128)} %get-tuple-element.380) | copy-start | bytes 52 | tf_op jit(solution)/shard_map/while
  173.9 5.2 %copy-start = (f32[4,1024,128,7]{2,1,3,0:T(8,128)}, f32[4,1024,128,7]{2,1,3,0:T(8,128)S(1)}, u32[]{:S(2)}) copy-start(f32[4,1024,128,7]{2,1,3,0:T(8,128)S(1)} %get-tuple-element.338) | copy-start | bytes 44040196 | tf_op jit(solution)/shard_map/while
  173.9 5.2 %copy-start.8 = (bf16[64,4,128]{2,1,0:T(4,128)(2,1)S(1)}, bf16[64,4,128]{2,1,0:T(4,128)(2,1)}, u32[]{:S(2)}) copy-start(bf16[64,4,128]{2,1,0:T(4,128)(2,1)} %get-tuple-element.385) | copy-start | bytes 196612 | tf_op jit(solution)/shard_map/while
  179.1 3.5 %copy-start.7 = (bf16[64,4,128]{2,1,0:T(4,128)(2,1)S(1)}, bf16[64,4,128]{2,1,0:T(4,128)(2,1)}, u32[]{:S(2)}) copy-start(bf16[64,4,128]{2,1,0:T(4,128)(2,1)} %get-tuple-element.386) | copy-start | bytes 196612 | tf_op jit(solution)/shard_map/while
  201.2 5.8 %copy-start.14 = (s32[4]{0:T(128)S(1)}, s32[4]{0:T(128)}, u32[]{:S(2)}) copy-start(s32[4]{0:T(128)} %get-tuple-element.380) | copy-start | bytes 52 | tf_op jit(solution)/shard_map/while
  212.7 5.2 %copy-start = (f32[4,1024,128,7]{2,1,3,0:T(8,128)}, f32[4,1024,128,7]{2,1,3,0:T(8,128)S(1)}, u32[]{:S(2)}) copy-start(f32[4,1024,128,7]{2,1,3,0:T(8,128)S(1)} %get-tuple-element.338) | copy-start | bytes 44040196 | tf_op jit(solution)/shard_map/while
  212.7 5.2 %copy-start.8 = (bf16[64,4,128]{2,1,0:T(4,128)(2,1)S(1)}, bf16[64,4,128]{2,1,0:T(4,128)(2,1)}, u32[]{:S(2)}) copy-start(bf16[64,4,128]{2,1,0:T(4,128)(2,1)} %get-tuple-element.385) | copy-start | bytes 196612 | tf_op jit(solution)/shard_map/while
  217.9 3.5 %copy-start.7 = (bf16[64,4,128]{2,1,0:T(4,128)(2,1)S(1)}, bf16[64,4,128]{2,1,0:T(4,128)(2,1)}, u32[]{:S(2)}) copy-start(bf16[64,4,128]{2,1,0:T(4,128)(2,1)} %get-tuple-element.386) | copy-start | bytes 196612 | tf_op jit(solution)/shard_map/while
  239.9 5.8 %copy-start.14 = (s32[4]{0:T(128)S(1)}, s32[4]{0:T(128)}, u32[]{:S(2)}) copy-start(s32[4]{0:T(128)} %get-tuple-element.380) | copy-start | bytes 52 | tf_op jit(solution)/shard_map/while
  251.4 5.2 %copy-start = (f32[4,1024,128,7]{2,1,3,0:T(8,128)}, f32[4,1024,128,7]{2,1,3,0:T(8,128)S(1)}, u32[]{:S(2)}) copy-start(f32[4,1024,128,7]{2,1,3,0:T(8,128)S(1)} %get-tuple-element.338) | copy-start | bytes 44040196 | tf_op jit(solution)/shard_map/while
  251.4 5.2 %copy-start.8 = (bf16[64,4,128]{2,1,0:T(4,128)(2,1)S(1)}, bf16[64,4,128]{2,1,0:T(4,128)(2,1)}, u32[]{:S(2)}) copy-start(bf16[64,4,128]{2,1,0:T(4,128)(2,1)} %get-tuple-element.385) | copy-start | bytes 196612 | tf_op jit(solution)/shard_map/while
  (26 other events, 63.4 us)
Sparse Core Ops, SparseCore 0:
  57.0 55.1 all-reduce.2
where the time goes:
time: 283 us; the launch traced here: 282 us
  local copies, waits for them, and re-layouts  72.7 us (26%)
  matrix products  72.5 us (26%)
  waiting for transfers between devices  70.4 us (25%)
  other arithmetic  23.2 us (8%)
  blocking collectives  17.8 us (6%)
  between operations  14.9 us (5%)
  starting transfers between devices  7.34 us (3%)
  loops' own time  2.99 us (1%)
    psum x1, waiting for transfers between devices, broadcast(): return lax.psum(kept, axis)  57.3 us
    dot_general x12, matrix products, group_part(): jnp.einsum('hgqk,khd->hgqd', weights.astype(jnp.bfloat16), per_head_value...  50.8 us
    dynamic_slice x40, local copies, waits for them, and re-layouts, per_device(): lax.map(attend, (query_all.reshape(blocks_here, rows_block, -1), every_ke...  40.5 us
    dot_general x12, matrix products, group_part(): jnp.einsum('qhgd,khd->hgqk', head_grouped, per_head_keys, preferred_eleme...  20.7 us
    reduce_sum x12, other arithmetic, group_part(): totals = jnp.sum(weights, axis=-1)  19.6 us
    all_to_all x1, waiting for transfers between devices, per_device(): lax.all_to_all(send_keys.reshape(devices, rows_block, kv_width), 'seq', s...  13.1 us
    dynamic_update_slice x8, local copies, waits for them, and re-layouts, per_device(): lax.map(attend, (query_all.reshape(blocks_here, rows_block, -1), every_ke...  9.99 us
    unnamed x1, blocking collectives  9.49 us
  transfers between devices with their start and end apart: 3, of which 2 were waited for; matrix products, arithmetic and copies ran while one was open for 3% of the time, Pallas kernels for 0%

commit v1 on v0

--- a/solution.py
+++ b/solution.py
@@ -13,7 +13,7 @@
 
 def broadcast(value, axis, source):
     kept = jnp.where(lax.axis_index(axis) == source, value, 0).astype(value.dtype)
-    return lax.psum(kept, axis)
+    return jnp.sum(lax.all_gather(kept, axis), axis=0)
 
 
 def group_part(query_row_list, key_row_list, value_row_list, visible):

time: 283 us -> 246 us (0.87)
  waiting for transfers between devices: 70.4 us -> 25.9 us
  local copies, waits for them, and re-layouts: 72.7 us -> 79 us
    psum x1 -> x0, waiting for transfers between devices: 57.3 us -> none  [broadcast(): return lax.psum(kept, axis)]
    all_to_all x1, waiting for transfers between devices: 0.01 us -> 15 us  [per_device(): lax.all_to_all(send_values.reshape(devices, rows_block, kv_width), 'seq',...]
    dynamic_slice x40, local copies, waits for them, and re-layouts: 40.5 us -> 46.8 us  [per_device(): lax.map(attend, (query_all.reshape(blocks_here, rows_block, -1), every_ke...]
    while x80 -> x64, local copies, waits for them, and re-layouts: 7.71 us -> 7.6 us
  transfers between devices with their start and end apart: 3 -> 3, of which waited for: 2 -> 2; matrix products, arithmetic and copies ran while one was open for 3% -> 4% of each run, Pallas kernels for 0% -> 0%
where the time goes in v1:
time: 246 us; the launch traced here: 245 us
  local copies, waits for them, and re-layouts  79 us (32%)
  matrix products  72.5 us (29%)
  waiting for transfers between devices  25.9 us (11%)
  other arithmetic  24.4 us (10%)
  blocking collectives  17.8 us (7%)
  between operations  14.8 us (6%)
  starting transfers between devices  7.34 us (3%)
  loops' own time  3.23 us (1%)
    dot_general x12, matrix products, group_part(): jnp.einsum('hgqk,khd->hgqd', weights.astype(jnp.bfloat16), per_head_value...  50.8 us
    dynamic_slice x40, local copies, waits for them, and re-layouts, per_device(): lax.map(attend, (query_all.reshape(blocks_here, rows_block, -1), every_ke...  46.8 us
    dot_general x12, matrix products, group_part(): jnp.einsum('qhgd,khd->hgqk', head_grouped, per_head_keys, preferred_eleme...  20.7 us
    reduce_sum x12, other arithmetic, group_part(): totals = jnp.sum(weights, axis=-1)  19.6 us
    all_to_all x1, waiting for transfers between devices, per_device(): lax.all_to_all(send_values.reshape(devices, rows_block, kv_width), 'seq',...  15 us
    all_to_all x1, waiting for transfers between devices, per_device(): lax.all_to_all(send_keys.reshape(devices, rows_block, kv_width), 'seq', s...  10.9 us
    dynamic_update_slice x8, local copies, waits for them, and re-layouts, per_device(): lax.map(attend, (query_all.reshape(blocks_here, rows_block, -1), every_ke...  9.99 us
    unnamed x1, blocking collectives  9.49 us
  transfers between devices with their start and end apart: 3, of which 2 were waited for; matrix products, arithmetic and copies ran while one was open for 4% of the time, Pallas kernels for 0%

profile of v1, /device:TPU:0, one launch (start us, length us, event | category | flops | bytes accessed | tf_op | source)
XLA Modules:
  0.0 244.9 jit_solution(15452786373149663998)
XLA Ops:
  9.2 9.5 %all-reduce = s32[32]{0:T(128)S(1)} all-reduce(s32[32]{0:T(128)S(1)} %bitcast_dynamic-update-slice_fusion), channel_id=3, replica_groups=mesh['samp'=4,'seq'=8] {'seq'}, use_global_device_ids=true, to_apply=%add | all-reduce | flops 32 | bytes 256
  18.8 8.3 %all-gather = s32[1,32,8]{2,0,1:T(1,128)S(1)} all-gather(s32[1,4,8]{2,0,1:T(1,128)} %bitcast.270), channel_id=2, replica_groups=mesh['samp'=4,'seq'=8] {'seq'}, dimensions={1}, use_global_device_ids=true | all-gather | bytes 1152 | tf_op jit(solution)/shard_map/all_gather | solution.py:71
  30.7 3.6 %all-to-all-start = ((bf16[8,128,512]{2,1,0:T(8,128)(2,1)}), bf16[8,128,512]{2,1,0:T(8,128)(2,1)S(1)}, u32[]{:S(2)}, u32[]{:S(2)}) async-start(bf16[8,128,512]{2,1,0:T(8,128)(2,1)} %copy.75), calls=%async_computation | async-start | bytes 2097152 | tf_op jit(solution)/shard_map/all_to_all | solution.py:91
  38.8 10.9 %all-to-all-done = bf16[8,128,512]{2,1,0:T(8,128)(2,1)S(1)} async-done(((bf16[8,128,512]{2,1,0:T(8,128)(2,1)}), bf16[8,128,512]{2,1,0:T(8,128)(2,1)S(1)}, u32[]{:S(2)}, u32[]{:S(2)}) %all-to-all-start) | async-done | bytes 1048608 | tf_op jit(solution)/shard_map/all_to_all | solution.py:91
  49.6 3.7 %all-to-all-start.1 = ((bf16[8,128,512]{2,1,0:T(8,128)(2,1)}), bf16[8,128,512]{2,1,0:T(8,128)(2,1)S(1)}, u32[]{:S(2)}, u32[]{:S(2)}) async-start(bf16[8,128,512]{2,1,0:T(8,128)(2,1)} %copy.76), calls=%async_computation.1 | async-start | bytes 2097152 | tf_op jit(solution)/shard_map/all_to_all | solution.py:98
  56.3 15.0 %all-to-all-done.1 = bf16[8,128,512]{2,1,0:T(8,128)(2,1)S(1)} async-done(((bf16[8,128,512]{2,1,0:T(8,128)(2,1)}), bf16[8,128,512]{2,1,0:T(8,128)(2,1)S(1)}, u32[]{:S(2)}, u32[]{:S(2)}) %all-to-all-start.1) | async-done | bytes 1048608 | tf_op jit(solution)/shard_map/all_to_all | solution.py:98
  71.3 2.8 %gather_fusion.1 = bf16[32,128,512]{2,1,0:T(8,128)(2,1)} fusion(bf16[8,128,512]{2,1,0:T(8,128)(2,1)S(1)} %all-to-all-done.1, s32[1024]{0:T(1024)S(1)} %pad_clamp_fusion), kind=kCustom, calls=%fused_computation.1 | custom fusion | bytes 8388736 | tf_op jit(solution)/shard_map/gather | solution.py:107
  76.9 161.2 %while.12 = (s32[]{:T(128)}, bf16[4,128,3584]{2,1,0:T(8,128)(2,1)}, bf16[4,128,3584]{2,1,0:T(8,128)(2,1)}, bf16[1,64,512]{2,1,0:T(8,128)(2,1)}, s32[4]{0:T(128)}...) while((s32[]{:T(128)}, bf16[4,128,3584]{2,1,0:T(8,128)(2,1)}, ...), condition=%wide.wide.region_10.11_spmd.clone, body=%wide.wide.region_3.10_spmd.clone.sunk | while | flops 2289687552 | bytes 159040496 | solution.py:129
  82.7 3.1 %constant_dynamic-slice_fusion.13 = (bf16[1,1024,512]{2,1,0:T(8,128)(2,1)}, bf16[1,1024,512]{2,1,0:T(8,128)(2,1)}) fusion(bf16[4,1024,512]{2,1,0:T(8,128)(2,1)} %get-tuple-element.386, s32[]{:T(128)} %get-tuple-element.361, bf16[4,1024,512]{2,1,0:T(8,128)(2,1)} %get-tuple-element.383), kind=kLoop, calls=%fused_computation.65.clone.clone.1 | loop fusion | bytes 4194308 | tf_op jit(solution)/shard_map/while/body/jit(dynamic_index_in_dim)/dynamic_slice | solution.py:129
  89.2 4.4 %bitcast_reduce_fusion.3 = (f32[4,7,128]{2,1,0:T(8,128)S(1)}, f32[4,1024,128,7]{2,1,3,0:T(8,128)S(1)}) fusion(pred[1024]{0:T(1024)(128)(4,1)S(1)} %fusion.129, bf16[1024,4,128,1]{0,2,3,1:T(8,128)(2,1)} %bitcast.254, bf16[128,4,7,128]{0,3,2,1:T(8,128)(2,1)S(1)} %bitcast.252), kind=kOutput, calls=%fused_computation.5.clone.clone.1 | convolution fusion | flops 950530560 | bytes 16661504 | tf_op jit(solution)/shard_map/while/body/eval_jaxpr/qhgd,khd->hgqk/dot_general | solution.py:25
  93.7 4.2 %fusion.130 = f32[4,7,128]{2,1,0:T(8,128)S(1)} fusion(f32[4,1024,128,7]{2,1,3,0:T(8,128)S(1)} %get-tuple-element.340, f32[4,7,128]{2,1,0:T(8,128)S(1)} %get-tuple-element.341, pred[1024]{0:T(1024)(128)(4,1)S(1)} %fusion.129), kind=kLoop, calls=%fused_computation.9.clone.clone.1 | loop fusion | flops 18346496 | bytes 14709760 | tf_op jit(solution)/shard_map/while/body/eval_jaxpr/reduce_sum | solution.py:31
  105.5 9.1 %fusion.134 = bf16[128,4,7,128]{0,3,2,1:T(8,128)(2,1)} fusion(f32[4,7,128,128]{2,3,1,0:T(8,128)S(1)} %copy-done.3, f32[4,7,128,128]{2,3,1,0:T(8,128)} %fusion.128, bf16[1024,4,128,1]{0,2,3,1:T(8,128)(2,1)S(1)} %bitcast.255, f32[4,1024,128,7]{2,1,3,0:T(8,128)} %copy-done, f32[4,7,128]{2,1,0:T(8,128)S(1)} %get-tuple-element.341, ...), kind=kOutput, calls=%fused_computation.17.clone.clone.1 | convolution fusion | flops 961085440 | bytes 20388864 | tf_op jit(solution)/shard_map/while/body/eval_jaxpr/hgqk,khd->hgqd/dot_general | solution.py:32
  123.0 3.1 %constant_dynamic-slice_fusion.13 = (bf16[1,1024,512]{2,1,0:T(8,128)(2,1)}, bf16[1,1024,512]{2,1,0:T(8,128)(2,1)}) fusion(bf16[4,1024,512]{2,1,0:T(8,128)(2,1)} %get-tuple-element.386, s32[]{:T(128)} %get-tuple-element.361, bf16[4,1024,512]{2,1,0:T(8,128)(2,1)} %get-tuple-element.383), kind=kLoop, calls=%fused_computation.65.clone.clone.1 | loop fusion | bytes 4194308 | tf_op jit(solution)/shard_map/while/body/jit(dynamic_index_in_dim)/dynamic_slice | solution.py:129
  129.5 4.4 %bitcast_reduce_fusion.3 = (f32[4,7,128]{2,1,0:T(8,128)S(1)}, f32[4,1024,128,7]{2,1,3,0:T(8,128)S(1)}) fusion(pred[1024]{0:T(1024)(128)(4,1)S(1)} %fusion.129, bf16[1024,4,128,1]{0,2,3,1:T(8,128)(2,1)} %bitcast.254, bf16[128,4,7,128]{0,3,2,1:T(8,128)(2,1)S(1)} %bitcast.252), kind=kOutput, calls=%fused_computation.5.clone.clone.1 | convolution fusion | flops 950530560 | bytes 16661504 | tf_op jit(solution)/shard_map/while/body/eval_jaxpr/qhgd,khd->hgqk/dot_general | solution.py:25
  133.9 4.2 %fusion.130 = f32[4,7,128]{2,1,0:T(8,128)S(1)} fusion(f32[4,1024,128,7]{2,1,3,0:T(8,128)S(1)} %get-tuple-element.340, f32[4,7,128]{2,1,0:T(8,128)S(1)} %get-tuple-element.341, pred[1024]{0:T(1024)(128)(4,1)S(1)} %fusion.129), kind=kLoop, calls=%fused_computation.9.clone.clone.1 | loop fusion | flops 18346496 | bytes 14709760 | tf_op jit(solution)/shard_map/while/body/eval_jaxpr/reduce_sum | solution.py:31
  145.8 9.1 %fusion.134 = bf16[128,4,7,128]{0,3,2,1:T(8,128)(2,1)} fusion(f32[4,7,128,128]{2,3,1,0:T(8,128)S(1)} %copy-done.3, f32[4,7,128,128]{2,3,1,0:T(8,128)} %fusion.128, bf16[1024,4,128,1]{0,2,3,1:T(8,128)(2,1)S(1)} %bitcast.255, f32[4,1024,128,7]{2,1,3,0:T(8,128)} %copy-done, f32[4,7,128]{2,1,0:T(8,128)S(1)} %get-tuple-element.341, ...), kind=kOutput, calls=%fused_computation.17.clone.clone.1 | convolution fusion | flops 961085440 | bytes 20388864 | tf_op jit(solution)/shard_map/while/body/eval_jaxpr/hgqk,khd->hgqd/dot_general | solution.py:32
  163.3 3.1 %constant_dynamic-slice_fusion.13 = (bf16[1,1024,512]{2,1,0:T(8,128)(2,1)}, bf16[1,1024,512]{2,1,0:T(8,128)(2,1)}) fusion(bf16[4,1024,512]{2,1,0:T(8,128)(2,1)} %get-tuple-element.386, s32[]{:T(128)} %get-tuple-element.361, bf16[4,1024,512]{2,1,0:T(8,128)(2,1)} %get-tuple-element.383), kind=kLoop, calls=%fused_computation.65.clone.clone.1 | loop fusion | bytes 4194308 | tf_op jit(solution)/shard_map/while/body/jit(dynamic_index_in_dim)/dynamic_slice | solution.py:129
  169.8 4.4 %bitcast_reduce_fusion.3 = (f32[4,7,128]{2,1,0:T(8,128)S(1)}, f32[4,1024,128,7]{2,1,3,0:T(8,128)S(1)}) fusion(pred[1024]{0:T(1024)(128)(4,1)S(1)} %fusion.129, bf16[1024,4,128,1]{0,2,3,1:T(8,128)(2,1)} %bitcast.254, bf16[128,4,7,128]{0,3,2,1:T(8,128)(2,1)S(1)} %bitcast.252), kind=kOutput, calls=%fused_computation.5.clone.clone.1 | convolution fusion | flops 950530560 | bytes 16661504 | tf_op jit(solution)/shard_map/while/body/eval_jaxpr/qhgd,khd->hgqk/dot_general | solution.py:25
  174.2 4.2 %fusion.130 = f32[4,7,128]{2,1,0:T(8,128)S(1)} fusion(f32[4,1024,128,7]{2,1,3,0:T(8,128)S(1)} %get-tuple-element.340, f32[4,7,128]{2,1,0:T(8,128)S(1)} %get-tuple-element.341, pred[1024]{0:T(1024)(128)(4,1)S(1)} %fusion.129), kind=kLoop, calls=%fused_computation.9.clone.clone.1 | loop fusion | flops 18346496 | bytes 14709760 | tf_op jit(solution)/shard_map/while/body/eval_jaxpr/reduce_sum | solution.py:31
  186.1 9.1 %fusion.134 = bf16[128,4,7,128]{0,3,2,1:T(8,128)(2,1)} fusion(f32[4,7,128,128]{2,3,1,0:T(8,128)S(1)} %copy-done.3, f32[4,7,128,128]{2,3,1,0:T(8,128)} %fusion.128, bf16[1024,4,128,1]{0,2,3,1:T(8,128)(2,1)S(1)} %bitcast.255, f32[4,1024,128,7]{2,1,3,0:T(8,128)} %copy-done, f32[4,7,128]{2,1,0:T(8,128)S(1)} %get-tuple-element.341, ...), kind=kOutput, calls=%fused_computation.17.clone.clone.1 | convolution fusion | flops 961085440 | bytes 20388864 | tf_op jit(solution)/shard_map/while/body/eval_jaxpr/hgqk,khd->hgqd/dot_general | solution.py:32
  203.6 3.1 %constant_dynamic-slice_fusion.13 = (bf16[1,1024,512]{2,1,0:T(8,128)(2,1)}, bf16[1,1024,512]{2,1,0:T(8,128)(2,1)}) fusion(bf16[4,1024,512]{2,1,0:T(8,128)(2,1)} %get-tuple-element.386, s32[]{:T(128)} %get-tuple-element.361, bf16[4,1024,512]{2,1,0:T(8,128)(2,1)} %get-tuple-element.383), kind=kLoop, calls=%fused_computation.65.clone.clone.1 | loop fusion | bytes 4194308 | tf_op jit(solution)/shard_map/while/body/jit(dynamic_index_in_dim)/dynamic_slice | solution.py:129
  210.1 4.4 %bitcast_reduce_fusion.3 = (f32[4,7,128]{2,1,0:T(8,128)S(1)}, f32[4,1024,128,7]{2,1,3,0:T(8,128)S(1)}) fusion(pred[1024]{0:T(1024)(128)(4,1)S(1)} %fusion.129, bf16[1024,4,128,1]{0,2,3,1:T(8,128)(2,1)} %bitcast.254, bf16[128,4,7,128]{0,3,2,1:T(8,128)(2,1)S(1)} %bitcast.252), kind=kOutput, calls=%fused_computation.5.clone.clone.1 | convolution fusion | flops 950530560 | bytes 16661504 | tf_op jit(solution)/shard_map/while/body/eval_jaxpr/qhgd,khd->hgqk/dot_general | solution.py:25
  214.5 4.2 %fusion.130 = f32[4,7,128]{2,1,0:T(8,128)S(1)} fusion(f32[4,1024,128,7]{2,1,3,0:T(8,128)S(1)} %get-tuple-element.340, f32[4,7,128]{2,1,0:T(8,128)S(1)} %get-tuple-element.341, pred[1024]{0:T(1024)(128)(4,1)S(1)} %fusion.129), kind=kLoop, calls=%fused_computation.9.clone.clone.1 | loop fusion | flops 18346496 | bytes 14709760 | tf_op jit(solution)/shard_map/while/body/eval_jaxpr/reduce_sum | solution.py:31
  226.4 9.1 %fusion.134 = bf16[128,4,7,128]{0,3,2,1:T(8,128)(2,1)} fusion(f32[4,7,128,128]{2,3,1,0:T(8,128)S(1)} %copy-done.3, f32[4,7,128,128]{2,3,1,0:T(8,128)} %fusion.128, bf16[1024,4,128,1]{0,2,3,1:T(8,128)(2,1)S(1)} %bitcast.255, f32[4,1024,128,7]{2,1,3,0:T(8,128)} %copy-done, f32[4,7,128]{2,1,0:T(8,128)S(1)} %get-tuple-element.341, ...), kind=kOutput, calls=%fused_computation.17.clone.clone.1 | convolution fusion | flops 961085440 | bytes 20388864 | tf_op jit(solution)/shard_map/while/body/eval_jaxpr/hgqk,khd->hgqd/dot_general | solution.py:32
  (181 shorter events, 89.7 us)
Async XLA Ops:
  6.5 28.4 %copy-start.4 = (bf16[1,512,512]{2,1,0:T(8,128)(2,1)S(1)}, bf16[1,512,512]{2,1,0:T(8,128)(2,1)}, u32[]{:S(2)}) copy-start(bf16[1,512,512]{2,1,0:T(8,128)(2,1)} %param.11) | copy-start | bytes 1572868
  30.7 19.0 %all-to-all-start = ((bf16[8,128,512]{2,1,0:T(8,128)(2,1)}), bf16[8,128,512]{2,1,0:T(8,128)(2,1)S(1)}, u32[]{:S(2)}, u32[]{:S(2)}) async-start(bf16[8,128,512]{2,1,0:T(8,128)(2,1)} %copy.75), calls=%async_computation | async-start | bytes 2097152 | tf_op jit(solution)/shard_map/all_to_all | solution.py:91
  34.2 39.9 %all-gather.4.cloned.1.call-start = ((), (), s32[]{:S(2)}) async-start(), calls=%async_computation.2 | async-start | bytes 1179648 | tf_op jit(solution)/shard_map/all_gather | solution.py:16
  35.8 17.6 %copy-start.10 = (s32[1,4,8]{2,1,0:T(4,128)S(1)}, s32[1,4,8]{2,1,0:T(4,128)}, u32[]{:S(2)}) copy-start(s32[1,4,8]{2,1,0:T(4,128)} %param.13) | copy-start | bytes 388
  49.6 21.6 %all-to-all-start.1 = ((bf16[8,128,512]{2,1,0:T(8,128)(2,1)}), bf16[8,128,512]{2,1,0:T(8,128)(2,1)S(1)}, u32[]{:S(2)}, u32[]{:S(2)}) async-start(bf16[8,128,512]{2,1,0:T(8,128)(2,1)} %copy.76), calls=%async_computation.1 | async-start | bytes 2097152 | tf_op jit(solution)/shard_map/all_to_all | solution.py:98
  82.2 5.8 %copy-start.11 = (s32[4]{0:T(128)S(1)}, s32[4]{0:T(128)}, u32[]{:S(2)}) copy-start(s32[4]{0:T(128)} %get-tuple-element.382) | copy-start | bytes 52 | tf_op jit(solution)/shard_map/while
  93.6 5.2 %copy-start = (f32[4,1024,128,7]{2,1,3,0:T(8,128)}, f32[4,1024,128,7]{2,1,3,0:T(8,128)S(1)}, u32[]{:S(2)}) copy-start(f32[4,1024,128,7]{2,1,3,0:T(8,128)S(1)} %get-tuple-element.340) | copy-start | bytes 44040196 | tf_op jit(solution)/shard_map/while
  93.6 5.2 %copy-start.7 = (bf16[64,4,128]{2,1,0:T(4,128)(2,1)S(1)}, bf16[64,4,128]{2,1,0:T(4,128)(2,1)}, u32[]{:S(2)}) copy-start(bf16[64,4,128]{2,1,0:T(4,128)(2,1)} %get-tuple-element.387) | copy-start | bytes 196612 | tf_op jit(solution)/shard_map/while
  98.8 3.5 %copy-start.6 = (bf16[64,4,128]{2,1,0:T(4,128)(2,1)S(1)}, bf16[64,4,128]{2,1,0:T(4,128)(2,1)}, u32[]{:S(2)}) copy-start(bf16[64,4,128]{2,1,0:T(4,128)(2,1)} %get-tuple-element.388) | copy-start | bytes 196612 | tf_op jit(solution)/shard_map/while
  102.3 3.2 %copy-start.3 = (f32[4,7,128,128]{2,3,1,0:T(8,128)S(1)}, f32[4,7,128,128]{2,3,1,0:T(8,128)}, u32[]{:S(2)}) copy-start(f32[4,7,128,128]{2,3,1,0:T(8,128)} %fusion.126) | copy-start | bytes 5505028 | tf_op jit(solution)/shard_map/while
  122.5 5.8 %copy-start.11 = (s32[4]{0:T(128)S(1)}, s32[4]{0:T(128)}, u32[]{:S(2)}) copy-start(s32[4]{0:T(128)} %get-tuple-element.382) | copy-start | bytes 52 | tf_op jit(solution)/shard_map/while
  133.9 5.2 %copy-start = (f32[4,1024,128,7]{2,1,3,0:T(8,128)}, f32[4,1024,128,7]{2,1,3,0:T(8,128)S(1)}, u32[]{:S(2)}) copy-start(f32[4,1024,128,7]{2,1,3,0:T(8,128)S(1)} %get-tuple-element.340) | copy-start | bytes 44040196 | tf_op jit(solution)/shard_map/while
  133.9 5.2 %copy-start.7 = (bf16[64,4,128]{2,1,0:T(4,128)(2,1)S(1)}, bf16[64,4,128]{2,1,0:T(4,128)(2,1)}, u32[]{:S(2)}) copy-start(bf16[64,4,128]{2,1,0:T(4,128)(2,1)} %get-tuple-element.387) | copy-start | bytes 196612 | tf_op jit(solution)/shard_map/while
  139.1 3.5 %copy-start.6 = (bf16[64,4,128]{2,1,0:T(4,128)(2,1)S(1)}, bf16[64,4,128]{2,1,0:T(4,128)(2,1)}, u32[]{:S(2)}) copy-start(bf16[64,4,128]{2,1,0:T(4,128)(2,1)} %get-tuple-element.388) | copy-start | bytes 196612 | tf_op jit(solution)/shard_map/while
  142.6 3.2 %copy-start.3 = (f32[4,7,128,128]{2,3,1,0:T(8,128)S(1)}, f32[4,7,128,128]{2,3,1,0:T(8,128)}, u32[]{:S(2)}) copy-start(f32[4,7,128,128]{2,3,1,0:T(8,128)} %fusion.126) | copy-start | bytes 5505028 | tf_op jit(solution)/shard_map/while
  162.8 5.8 %copy-start.11 = (s32[4]{0:T(128)S(1)}, s32[4]{0:T(128)}, u32[]{:S(2)}) copy-start(s32[4]{0:T(128)} %get-tuple-element.382) | copy-start | bytes 52 | tf_op jit(solution)/shard_map/while
  174.2 5.2 %copy-start = (f32[4,1024,128,7]{2,1,3,0:T(8,128)}, f32[4,1024,128,7]{2,1,3,0:T(8,128)S(1)}, u32[]{:S(2)}) copy-start(f32[4,1024,128,7]{2,1,3,0:T(8,128)S(1)} %get-tuple-element.340) | copy-start | bytes 44040196 | tf_op jit(solution)/shard_map/while
  174.2 5.2 %copy-start.7 = (bf16[64,4,128]{2,1,0:T(4,128)(2,1)S(1)}, bf16[64,4,128]{2,1,0:T(4,128)(2,1)}, u32[]{:S(2)}) copy-start(bf16[64,4,128]{2,1,0:T(4,128)(2,1)} %get-tuple-element.387) | copy-start | bytes 196612 | tf_op jit(solution)/shard_map/while
  179.4 3.5 %copy-start.6 = (bf16[64,4,128]{2,1,0:T(4,128)(2,1)S(1)}, bf16[64,4,128]{2,1,0:T(4,128)(2,1)}, u32[]{:S(2)}) copy-start(bf16[64,4,128]{2,1,0:T(4,128)(2,1)} %get-tuple-element.388) | copy-start | bytes 196612 | tf_op jit(solution)/shard_map/while
  182.9 3.2 %copy-start.3 = (f32[4,7,128,128]{2,3,1,0:T(8,128)S(1)}, f32[4,7,128,128]{2,3,1,0:T(8,128)}, u32[]{:S(2)}) copy-start(f32[4,7,128,128]{2,3,1,0:T(8,128)} %fusion.126) | copy-start | bytes 5505028 | tf_op jit(solution)/shard_map/while
  203.1 5.8 %copy-start.11 = (s32[4]{0:T(128)S(1)}, s32[4]{0:T(128)}, u32[]{:S(2)}) copy-start(s32[4]{0:T(128)} %get-tuple-element.382) | copy-start | bytes 52 | tf_op jit(solution)/shard_map/while
  214.5 5.2 %copy-start = (f32[4,1024,128,7]{2,1,3,0:T(8,128)}, f32[4,1024,128,7]{2,1,3,0:T(8,128)S(1)}, u32[]{:S(2)}) copy-start(f32[4,1024,128,7]{2,1,3,0:T(8,128)S(1)} %get-tuple-element.340) | copy-start | bytes 44040196 | tf_op jit(solution)/shard_map/while
  214.5 5.2 %copy-start.7 = (bf16[64,4,128]{2,1,0:T(4,128)(2,1)S(1)}, bf16[64,4,128]{2,1,0:T(4,128)(2,1)}, u32[]{:S(2)}) copy-start(bf16[64,4,128]{2,1,0:T(4,128)(2,1)} %get-tuple-element.387) | copy-start | bytes 196612 | tf_op jit(solution)/shard_map/while
  219.7 3.5 %copy-start.6 = (bf16[64,4,128]{2,1,0:T(4,128)(2,1)S(1)}, bf16[64,4,128]{2,1,0:T(4,128)(2,1)}, u32[]{:S(2)}) copy-start(bf16[64,4,128]{2,1,0:T(4,128)(2,1)} %get-tuple-element.388) | copy-start | bytes 196612 | tf_op jit(solution)/shard_map/while
  (15 other events, 27.8 us)
Sparse Core Ops, SparseCore 0:
  36.9 31.0 all-gather.3
